TPU v7x, 32 devices: a whole 2x2x4 slice. The times are simulated.
32 devices in a mesh: dp: 4 (over x, core), ctx: 8 (over z, y).
Axes of the slice: x: 2, y: 2, z: 4, core: 2. Of those that a mesh axis runs over, the one named last changes fastest.
Arguments:
- grad_output: bfloat16 [4, 2048, 1024], P('dp', None, 'ctx'), may hold values from -6 to 6
- post_gate: bfloat16 [4, 2048, 1024], P('dp', None, 'ctx'), may hold values from -6 to 6
- pre_gate: bfloat16 [4, 2048, 1024], P('dp', None, 'ctx'), may hold values from -6 to 6
- value_branch: bfloat16 [4, 2048, 1024], P('dp', None, 'ctx'), may hold values from -6 to 6
- long_filter: float32 [2048, 1024], P('ctx'), may hold values from -0.1875 to 0.1875
- skip_weight: float32 [2048], replicated, may hold values from -3 to 3
Outputs:
- grad_pre_gate: bfloat16 [4, 2048, 1024], P('dp', None, 'ctx')
- grad_value_branch: bfloat16 [4, 2048, 1024], P('dp', None, 'ctx')
- grad_long_filter: float32 [2048, 1024], P('ctx', 'dp')
All inputs are finite; a program needn't handle non-finite values.
Results may differ from a plain program's by a relative error of at most 0.0095.
Values may be sent and summed in bfloat16 or wider, within the bound.
No kernel may reach another device: no remote copies, remote signals or barrier semaphores. Data moves between devices by JAX's collectives and lax.ppermute only.
A program may use at most 64 MiB of HBM per device.

v0:
```python
import math

import jax
import jax.numpy as jnp
import numpy as np
from jax import lax
from jax.experimental import pallas as pl
from jax.experimental.pallas import tpu as pltpu
from jax.sharding import PartitionSpec as P

highest = lax.Precision.HIGHEST
f32 = jnp.float32
bf16 = jnp.bfloat16
LANES = 128
STEP = 32


def tables(length):
    freq = np.arange(length)
    hi = (np.arange(length // STEP)[:, None] * STEP * freq) % (2 * length)
    lo = (np.arange(STEP)[:, None] * freq) % (2 * length)
    scale = math.pi / length
    pack = lambda p: np.stack([np.cos(p * scale), np.sin(p * scale)]).astype(np.float32)
    return pack(hi), pack(lo)


def product_kernel(go_ref, po_ref, pr_ref, vb_ref, out_ref):
    out_ref[0, 0] = (go_ref[0].astype(f32) * po_ref[0].astype(f32)).astype(bf16)
    out_ref[0, 1] = (pr_ref[0].astype(f32) * vb_ref[0].astype(f32)).astype(bf16)


def product(grad_output, post_gate, pre_gate, value_branch, groups):
    _, channels, block = grad_output.shape
    rows = channels // groups
    spec = pl.BlockSpec((1, rows, block), lambda i: (0, i, 0))
    return pl.pallas_call(
        product_kernel,
        grid=(groups,),
        in_specs=[spec] * 4,
        out_specs=pl.BlockSpec((1, 2, rows, block), lambda i: (i, 0, 0, 0)),
        out_shape=jax.ShapeDtypeStruct((groups, 2, rows, block), bf16),
        cost_estimate=pl.CostEstimate(
            flops=2 * channels * block, bytes_accessed=12 * channels * block, transcendentals=0
        ),
        name="product",
    )(grad_output, post_gate, pre_gate, value_branch)


def filter_kernel(filt_ref, hi_ref, lo_ref, w_ref, spec_ref):
    n = pl.program_id(0)
    length = filt_ref.shape[1]
    lo_cos = lo_ref[0]
    lo_sin = lo_ref[1]
    lane = lax.broadcasted_iota(jnp.int32, (STEP, LANES), 1)
    row = lax.broadcasted_iota(jnp.int32, (STEP, LANES), 0)
    first = jnp.logical_and(lane == 0, n == 0)
    nyquist = jnp.where(row % 2 == 0, 1.0, -1.0).astype(f32)
    for i in range(length // STEP):
        hi_cos = hi_ref[0, i : i + 1, :]
        hi_sin = hi_ref[1, i : i + 1, :]
        cosine = hi_cos * lo_cos - hi_sin * lo_sin
        sine = hi_sin * lo_cos + hi_cos * lo_sin
        rows = pl.ds(i * STEP, STEP)
        w_ref[rows, :LANES] = cosine.astype(bf16)
        w_ref[rows, LANES:] = jnp.where(first, nyquist, -sine).astype(bf16)
    spec_ref[...] = jnp.dot(
        filt_ref[...].astype(bf16), w_ref[...], preferred_element_type=f32
    )


def filter_spectrum_dense(filt):
    channels, length = filt.shape
    hi, lo = tables(length)
    tiles = length // LANES
    return pl.pallas_call(
        filter_kernel,
        grid=(tiles,),
        in_specs=[
            pl.BlockSpec((channels, length), lambda n: (0, 0)),
            pl.BlockSpec((2, length // STEP, LANES), lambda n: (0, 0, n)),
            pl.BlockSpec((2, STEP, LANES), lambda n: (0, 0, n)),
        ],
        out_specs=[
            pl.BlockSpec((length, 2 * LANES), lambda n: (0, n)),
            pl.BlockSpec((channels, 2 * LANES), lambda n: (0, n)),
        ],
        out_shape=[
            jax.ShapeDtypeStruct((length, 2 * length), bf16),
            jax.ShapeDtypeStruct((channels, 2 * length), f32),
        ],
        compiler_params=pltpu.CompilerParams(vmem_limit_bytes=16 * 2**20),
        cost_estimate=pl.CostEstimate(
            flops=4 * channels * length * length,
            bytes_accessed=4 * channels * length * 3 + 4 * length * length,
            transcendentals=0,
        ),
        name="filter_spectrum",
    )(filt, jnp.asarray(hi), jnp.asarray(lo))


def correlate_kernel(got_ref, w_ref, spec_ref, corr_ref, grad_ref, rows_ref, prod_ref):
    groups, _, channels, block = got_ref.shape
    length = groups * block
    for p in range(groups):
        cols = pl.ds(p * block, block)
        rows_ref[:channels, cols] = got_ref[p, 0]
        rows_ref[channels:, cols] = got_ref[p, 1]
    lane = lax.broadcasted_iota(jnp.int32, (channels, LANES), 1)
    for n in range(length // LANES):
        re = pl.ds(2 * n * LANES, LANES)
        im = pl.ds((2 * n + 1) * LANES, LANES)
        both = pl.ds(2 * n * LANES, 2 * LANES)
        spectrum = jnp.dot(rows_ref[...], w_ref[:, both], preferred_element_type=f32)
        g_re = spectrum[:channels, :LANES]
        g_im = spectrum[:channels, LANES:]
        s_re = spectrum[channels:, :LANES]
        s_im = spectrum[channels:, LANES:]
        h_re = spec_ref[:, re]
        h_im = spec_ref[:, im]
        for y_re, y_im, at in ((h_re, h_im, 0), (s_re, s_im, channels)):
            rr = g_re * y_re
            ii = g_im * y_im
            cross = g_im * y_re - g_re * y_im
            scale = 1.0 / length
            if n == 0:
                first = lane == 0
                real = jnp.where(first, rr, rr + ii)
                imag = jnp.where(first, ii, cross)
                scale = jnp.where(first, 0.5 / length, 1.0 / length)
            else:
                real = rr + ii
                imag = cross
            out = pl.ds(at, channels)
            prod_ref[out, re] = (real * scale).astype(bf16)
            prod_ref[out, im] = (imag * scale).astype(bf16)
    taps = grad_ref.shape[2]
    tile = 2 * LANES
    for q in range(length // tile):
        out = lax.dot_general(
            prod_ref[...],
            w_ref[pl.ds(q * tile, tile), :],
            (((1,), (1,)), ((), ())),
            preferred_element_type=f32,
        )
        for part in range(tile // block):
            corr_ref[q * (tile // block) + part] = out[
                :channels, part * block : (part + 1) * block
            ].astype(bf16)
        start = q * tile
        grad_ref[start // taps, :, pl.ds(start % taps, tile)] = out[channels:].astype(bf16)


def correlate_dense(got, w, spec, shares):
    groups, _, channels, block = got.shape
    length = groups * block
    vmem = pl.BlockSpec(memory_space=pltpu.VMEM)
    return pl.pallas_call(
        correlate_kernel,
        in_specs=[vmem] * 3,
        out_specs=[vmem] * 2,
        out_shape=[
            jax.ShapeDtypeStruct((groups, channels, block), bf16),
            jax.ShapeDtypeStruct((shares, channels, length // shares), bf16),
        ],
        scratch_shapes=[
            pltpu.VMEM((2 * channels, length), bf16),
            pltpu.VMEM((2 * channels, 2 * length), bf16),
        ],
        compiler_params=pltpu.CompilerParams(vmem_limit_bytes=32 * 2**20),
        cost_estimate=pl.CostEstimate(
            flops=16 * channels * length * length,
            bytes_accessed=4 * length * length + 20 * channels * length,
            transcendentals=0,
        ),
        name="correlate",
    )(got, w, spec)


def shards_dense(grad_output, post_gate, pre_gate, value_branch, long_filter, skip_weight):
    groups = lax.axis_size("ctx")
    shares = lax.axis_size("dp")
    seqs, channels, block = grad_output.shape
    length = long_filter.shape[1]
    token_count = seqs * shares * length
    sent = product(grad_output, post_gate, pre_gate, value_branch, groups)
    w, spec = filter_spectrum_dense(long_filter)
    got = lax.all_to_all(sent, "ctx", split_axis=0, concat_axis=0, tiled=True)
    corr, grad = correlate_dense(got, w, spec, shares)
    back = lax.all_to_all(corr, "ctx", split_axis=0, concat_axis=0, tiled=True)
    terms = lax.all_to_all(grad, "dp", split_axis=0, concat_axis=0, tiled=True)
    returned = back.reshape(seqs, channels, block)
    gated = (grad_output.astype(f32) * post_gate.astype(f32)).astype(bf16)
    summed = returned.astype(f32) + skip_weight[None, :, None] * gated.astype(f32)
    grad_pre_gate = (summed * value_branch.astype(f32)).astype(bf16)
    grad_value_branch = (summed * pre_gate.astype(f32)).astype(bf16)
    grad_long_filter = jnp.sum(terms.astype(f32), axis=0) * (1.0 / math.sqrt(token_count))
    return (grad_pre_gate, grad_value_branch, grad_long_filter)


def split_factor(length):
    for candidate in range(128, 1, -1):
        if length % candidate == 0:
            return candidate
    return 1


def twiddle(row_count, col_count, modulus, sign_value):
    row_index = lax.broadcasted_iota(jnp.int32, (row_count, col_count), 0)
    col_index = lax.broadcasted_iota(jnp.int32, (row_count, col_count), 1)
    phases = row_index * col_index % modulus
    angles = phases.astype(jnp.float32) * (2.0 * math.pi / modulus)
    return (jnp.cos(angles), sign_value * jnp.sin(angles))


def block_matrix(row_count, col_count, modulus, sign_value, part_count):
    cosine, sine = twiddle(row_count, col_count, modulus, sign_value)
    matrix = jnp.stack([jnp.stack([cosine, sine], 1), jnp.stack([-sine, cosine], 1)], 0)
    return matrix[:part_count]


def transform(parts, sign_value, length):
    part_count = parts.shape[0]
    width = parts.shape[-1]
    leading = split_factor(length)
    if length <= 256 or leading == 1 or leading == length:
        matrix = block_matrix(width, length, length, sign_value, part_count)
        return jnp.einsum("p...j,pjqk->q...k", parts, matrix, precision=highest)
    trailing = length // leading
    live = -(-width // trailing)
    if live * trailing != width:
        extra = [(0, 0)] * (parts.ndim - 1) + [(0, live * trailing - width)]
        parts = jnp.pad(parts, extra)
    batch_dims = parts.shape[1:-1]
    parts = parts.reshape((part_count,) + batch_dims + (live, trailing))
    matrix = block_matrix(live, leading, leading, sign_value, part_count)
    first = jnp.einsum("p...jb,pjqk->q...kb", parts, matrix, precision=highest)
    turn_cos, turn_sin = twiddle(leading, trailing, length, sign_value)
    rotated = jnp.stack(
        [first[0] * turn_cos - first[1] * turn_sin, first[0] * turn_sin + first[1] * turn_cos], 0
    )
    deep = transform(rotated, sign_value, trailing)
    return jnp.swapaxes(deep, -1, -2).reshape((2,) + batch_dims + (length,))


def mirror(values):
    return jnp.roll(jnp.flip(values, -1), 1, -1)


def filter_spectrum(filter_rows):
    length = filter_rows.shape[1]
    spectrum = transform(filter_rows[None], -1.0, 2 * length)
    return (spectrum[0], spectrum[1])


def correlate(grad_rows, saved_rows, filt_real, filt_imag):
    length = grad_rows.shape[2]
    padded = 2 * length
    stacked = jnp.stack([grad_rows.astype(jnp.float32), saved_rows.astype(jnp.float32)], 0)
    spectrum = transform(stacked, -1.0, padded)
    spec_real = spectrum[0]
    spec_imag = spectrum[1]
    flip_real = mirror(spec_real)
    flip_imag = mirror(spec_imag)
    grad_real = 0.5 * (spec_real + flip_real)
    grad_imag = 0.5 * (spec_imag - flip_imag)
    input_real = 0.5 * (spec_imag + flip_imag)
    input_imag = 0.5 * (flip_real - spec_real)
    first_real = filt_real * grad_real + filt_imag * grad_imag
    first_imag = filt_real * grad_imag - filt_imag * grad_real
    second_real = grad_real * input_real + grad_imag * input_imag
    second_imag = grad_imag * input_real - grad_real * input_imag
    combined = jnp.stack([first_real - second_imag, first_imag + second_real], 0)
    result = transform(combined, 1.0, padded)
    factor = 1.0 / padded
    correlated = (result[0, ..., :length] * factor).astype(jnp.bfloat16)
    filter_terms = result[1, ..., :length] * factor
    return (correlated, filter_terms)


def shards_long(grad_output, post_gate, pre_gate, value_branch, long_filter, skip_weight):
    seq_count = grad_output.shape[0]
    length = long_filter.shape[1]
    token_count = seq_count * lax.axis_size("dp") * length
    gated = (grad_output.astype(jnp.float32) * post_gate.astype(jnp.float32)).astype(jnp.bfloat16)
    saved = (pre_gate.astype(jnp.float32) * value_branch.astype(jnp.float32)).astype(jnp.bfloat16)
    filt_real, filt_imag = filter_spectrum(long_filter)
    correlated, filter_terms = correlate(
        lax.all_to_all(gated, "ctx", split_axis=1, concat_axis=2, tiled=True),
        lax.all_to_all(saved, "ctx", split_axis=1, concat_axis=2, tiled=True),
        filt_real,
        filt_imag,
    )
    back = lax.all_to_all(correlated, "ctx", split_axis=2, concat_axis=1, tiled=True)
    returned, filter_terms = (back, filter_terms)
    filter_sum = jnp.sum(filter_terms, axis=0)
    shares = lax.psum_scatter(
        filter_sum.astype(jnp.bfloat16), "dp", scatter_dimension=1, tiled=True
    ).astype(jnp.float32)
    summed = returned.astype(jnp.float32) + skip_weight[None, :, None] * gated.astype(jnp.float32)
    grad_pre_gate = (summed * value_branch.astype(jnp.float32)).astype(jnp.bfloat16)
    grad_value_branch = (summed * pre_gate.astype(jnp.float32)).astype(jnp.bfloat16)
    grad_long_filter = shares * (1.0 / math.sqrt(token_count))
    return (grad_pre_gate, grad_value_branch, grad_long_filter)


def shards(grad_output, post_gate, pre_gate, value_branch, long_filter, skip_weight):
    seqs, _, block = grad_output.shape
    rows, length = long_filter.shape
    shares = lax.axis_size("dp")
    dense = (
        seqs == 1
        and length <= 1024
        and block == LANES
        and rows % 16 == 0
        and length % (2 * LANES * shares) == 0
    )
    body = shards_dense if dense else shards_long
    return body(grad_output, post_gate, pre_gate, value_branch, long_filter, skip_weight)


def solution(mesh):
    return jax.shard_map(
        shards,
        mesh=mesh,
        in_specs=(
            P("dp", None, "ctx"),
            P("dp", None, "ctx"),
            P("dp", None, "ctx"),
            P("dp", None, "ctx"),
            P("ctx", None),
            P(),
        ),
        out_specs=(P("dp", None, "ctx"), P("dp", None, "ctx"), P("ctx", "dp")),
        check_vma=False,
    )
```

profile of v0, /device:TPU:0, one launch (start us, length us, event | category | flops | bytes accessed | tf_op | source)
XLA Modules:
  0.0 80.4 jit_solution(13612027076029117814)
XLA Ops:
  0.6 0.0 copy-start.1
  0.6 0.0 copy-start.2
  0.7 0.0 copy-start
  0.7 5.5 %product.1 = bf16[8,2,256,128]{3,2,1,0:T(8,128)(2,1)} custom-call(bf16[1,2048,128]{2,1,0:T(8,128)(2,1)} %go_ref.1, bf16[1,2048,128]{2,1,0:T(8,128)(2,1)} %po_ref.1, bf16[1,2048,128]{2,1,0:T(8,128)(2,1)} %pr_ref.1, bf16[1,2048,128]{2,1,0:T(8,128)(2,1)} %vb_ref.1), custom_call_target="tpu_custom_call" | custom-call | flops 524288 | bytes 3145728 | tf_op jit(solution)/shard_map/product/pallas_call | solution.py:36
  6.2 7.3 %all-to-all-start = ((bf16[8,2,256,128]{3,2,1,0:T(8,128)(2,1)}), bf16[8,2,256,128]{3,2,1,0:T(8,128)(2,1)S(1)}, u32[]{:S(2)}, u32[]{:S(2)}) async-start(bf16[8,2,256,128]{3,2,1,0:T(8,128)(2,1)} %product.1), calls=%async_computation | async-start | bytes 2097152 | tf_op jit(solution)/shard_map/all_to_all | solution.py:187
  13.5 0.0 copy-done.1
  13.5 0.0 copy-done.2
  13.5 0.0 copy-done
  13.5 4.6 %filter_spectrum.1 = (bf16[1024,2048]{1,0:T(8,128)(2,1)S(1)}, f32[256,2048]{1,0:T(8,128)S(1)}) custom-call(f32[256,1024]{1,0:T(8,128)S(1)} %copy-done, f32[2,32,1024]{2,1,0:T(8,128)S(1)} %copy-done.2, f32[2,32,1024]{2,1,0:T(8,128)S(1)} %copy-done.1), custom_call_target="tpu_custom_call" | custom-call | flops 1073741824 | bytes 7340032 | tf_op jit(solution)/shard_map/filter_spectrum/pallas_call | solution.py:75
  18.1 0.0 copy-start.3
  18.1 1.9 %copy-done.3 = bf16[1024,2048]{1,0:T(8,128)(2,1)} copy-done((bf16[1024,2048]{1,0:T(8,128)(2,1)}, bf16[1024,2048]{1,0:T(8,128)(2,1)S(1)}, u32[]{:S(2)}) %copy-start.3) | copy-done | bytes 4194328
  20.1 0.0 copy-start.5
  20.1 1.3 %copy-done.5 = f32[256,2048]{1,0:T(8,128)} copy-done((f32[256,2048]{1,0:T(8,128)}, f32[256,2048]{1,0:T(8,128)S(1)}, u32[]{:S(2)}) %copy-start.5) | copy-done | bytes 2097176
  21.4 17.9 %all-to-all-done.got_ref = bf16[8,2,256,128]{3,2,1,0:T(8,128)(2,1)S(1)} async-done(((bf16[8,2,256,128]{3,2,1,0:T(8,128)(2,1)}), bf16[8,2,256,128]{3,2,1,0:T(8,128)(2,1)S(1)}, u32[]{:S(2)}, u32[]{:S(2)}) %all-to-all-start) | async-done | bytes 1048608 | tf_op jit(solution)/shard_map/all_to_all | solution.py:187
  39.3 0.0 copy-start.4
  39.3 2.2 %copy-done.4 = bf16[1024,2048]{1,0:T(8,128)(2,1)S(1)} copy-done((bf16[1024,2048]{1,0:T(8,128)(2,1)S(1)}, bf16[1024,2048]{1,0:T(8,128)(2,1)}, u32[]{:S(2)}) %copy-start.4) | copy-done | bytes 4194328
  41.5 0.0 copy-start.6
  41.5 1.6 %copy-done.6 = f32[256,2048]{1,0:T(8,128)S(1)} copy-done((f32[256,2048]{1,0:T(8,128)S(1)}, f32[256,2048]{1,0:T(8,128)}, u32[]{:S(2)}) %copy-start.6) | copy-done | bytes 2097176
  43.1 0.0 copy-start.7
  43.1 0.0 copy-start.8
  43.1 0.0 copy-start.9
  43.1 5.4 %correlate.1 = (bf16[8,256,128]{2,1,0:T(8,128)(2,1)}, bf16[4,256,256]{2,1,0:T(8,128)(2,1)S(1)}) custom-call(bf16[8,2,256,128]{3,2,1,0:T(8,128)(2,1)S(1)} %all-to-all-done.got_ref, bf16[1024,2048]{1,0:T(8,128)(2,1)S(1)} %copy-done.4, f32[256,2048]{1,0:T(8,128)S(1)} %copy-done.6), custom_call_target="tpu_custom_call" | custom-call | flops 4294967296 | bytes 9437184 | tf_op jit(solution)/shard_map/correlate/pallas_call | solution.py:157
  48.5 11.4 %all_to_all.15 = bf16[4,256,256]{2,1,0:T(8,128)(2,1)S(1)} all-to-all(bf16[4,256,256]{2,1,0:T(8,128)(2,1)S(1)} %get-tuple-element.10), channel_id=1, replica_groups=mesh['dp'=4,'ctx'=8] {'dp'}, dimensions={0} | all-to-all | bytes 1048576 | tf_op jit(solution)/shard_map/all_to_all | solution.py:190
  59.9 3.6 %all-to-all-start.1 = ((bf16[8,256,128]{2,1,0:T(8,128)(2,1)}), bf16[8,256,128]{2,1,0:T(8,128)(2,1)S(1)}, u32[]{:S(2)}, u32[]{:S(2)}) async-start(bf16[8,256,128]{2,1,0:T(8,128)(2,1)} %get-tuple-element.9), calls=%async_computation.1 | async-start | bytes 1048576 | tf_op jit(solution)/shard_map/all_to_all | solution.py:189
  63.5 0.1 convert_reduce_fusion
  63.5 0.7 broadcast_multiply_fusion
  64.2 13.5 %all-to-all-done.1 = bf16[8,256,128]{2,1,0:T(8,128)(2,1)S(1)} async-done(((bf16[8,256,128]{2,1,0:T(8,128)(2,1)}), bf16[8,256,128]{2,1,0:T(8,128)(2,1)S(1)}, u32[]{:S(2)}, u32[]{:S(2)}) %all-to-all-start.1) | async-done | bytes 524320 | tf_op jit(solution)/shard_map/all_to_all | solution.py:189
  77.7 0.0 copy-done.7
  77.7 0.0 copy-done.8
  77.7 0.0 copy-done.9
  77.7 2.6 %multiply_convert_fusion = (bf16[1,2048,128]{2,1,0:T(8,128)(2,1)}, bf16[1,2048,128]{2,1,0:T(8,128)(2,1)}) fusion(bf16[1,2048,128]{2,1,0:T(8,128)(2,1)S(1)} %copy-done.7, f32[2048]{0:T(1024)S(1)} %copy-done.9, bf16[1,2048,128]{2,1,0:T(8,128)(2,1)S(1)} %copy-done.8, bf16[1,2048,128]{2,1,0:T(8,128)(2,1)} %go_ref.1, bf16[1,2048,128]{2,1,0:T(8,128)(2,1)} %vb_ref.1, ...), kind=kLoop, calls=%fused_computation.2 | loop fusion | flops 3670016 | bytes 3678208 | tf_op jit(solution)/shard_map/convert_element_type | solution.py:195
Async XLA Ops:
  0.6 12.9 %copy-start.1 = (f32[2,32,1024]{2,1,0:T(8,128)S(1)}, f32[2,32,1024]{2,1,0:T(8,128)}, u32[]{:S(2)}) copy-start(f32[2,32,1024]{2,1,0:T(8,128)} %constant.9.clone.lo_ref) | copy-start | bytes 786436
  0.6 12.9 %copy-start.2 = (f32[2,32,1024]{2,1,0:T(8,128)S(1)}, f32[2,32,1024]{2,1,0:T(8,128)}, u32[]{:S(2)}) copy-start(f32[2,32,1024]{2,1,0:T(8,128)} %constant.8.clone.hi_ref) | copy-start | bytes 786436
  0.7 12.9 %copy-start = (f32[256,1024]{1,0:T(8,128)S(1)}, f32[256,1024]{1,0:T(8,128)}, u32[]{:S(2)}) copy-start(f32[256,1024]{1,0:T(8,128)} %filt_ref.1) | copy-start | bytes 3145732
  6.2 33.1 %all-to-all-start = ((bf16[8,2,256,128]{3,2,1,0:T(8,128)(2,1)}), bf16[8,2,256,128]{3,2,1,0:T(8,128)(2,1)S(1)}, u32[]{:S(2)}, u32[]{:S(2)}) async-start(bf16[8,2,256,128]{3,2,1,0:T(8,128)(2,1)} %product.1), calls=%async_computation | async-start | bytes 2097152 | tf_op jit(solution)/shard_map/all_to_all | solution.py:187
  18.1 1.9 %copy-start.3 = (bf16[1024,2048]{1,0:T(8,128)(2,1)}, bf16[1024,2048]{1,0:T(8,128)(2,1)S(1)}, u32[]{:S(2)}) copy-start(bf16[1024,2048]{1,0:T(8,128)(2,1)S(1)} %get-tuple-element.7.w_ref) | copy-start | bytes 12582916
  20.1 1.3 %copy-start.5 = (f32[256,2048]{1,0:T(8,128)}, f32[256,2048]{1,0:T(8,128)S(1)}, u32[]{:S(2)}) copy-start(f32[256,2048]{1,0:T(8,128)S(1)} %get-tuple-element.8.spec_ref) | copy-start | bytes 6291460
  39.3 2.2 %copy-start.4 = (bf16[1024,2048]{1,0:T(8,128)(2,1)S(1)}, bf16[1024,2048]{1,0:T(8,128)(2,1)}, u32[]{:S(2)}) copy-start(bf16[1024,2048]{1,0:T(8,128)(2,1)} %copy-done.3) | copy-start | bytes 12582916
  41.5 1.6 %copy-start.6 = (f32[256,2048]{1,0:T(8,128)S(1)}, f32[256,2048]{1,0:T(8,128)}, u32[]{:S(2)}) copy-start(f32[256,2048]{1,0:T(8,128)} %copy-done.5) | copy-start | bytes 6291460
  43.1 34.6 %copy-start.7 = (bf16[1,2048,128]{2,1,0:T(8,128)(2,1)S(1)}, bf16[1,2048,128]{2,1,0:T(8,128)(2,1)}, u32[]{:S(2)}) copy-start(bf16[1,2048,128]{2,1,0:T(8,128)(2,1)} %pr_ref.1) | copy-start | bytes 1572868
  43.1 34.6 %copy-start.8 = (bf16[1,2048,128]{2,1,0:T(8,128)(2,1)S(1)}, bf16[1,2048,128]{2,1,0:T(8,128)(2,1)}, u32[]{:S(2)}) copy-start(bf16[1,2048,128]{2,1,0:T(8,128)(2,1)} %po_ref.1) | copy-start | bytes 1572868
  43.1 34.6 %copy-start.9 = (f32[2048]{0:T(1024)S(1)}, f32[2048]{0:T(1024)}, u32[]{:S(2)}) copy-start(f32[2048]{0:T(1024)} %param.13) | copy-start | bytes 24580
  59.9 17.8 %all-to-all-start.1 = ((bf16[8,256,128]{2,1,0:T(8,128)(2,1)}), bf16[8,256,128]{2,1,0:T(8,128)(2,1)S(1)}, u32[]{:S(2)}, u32[]{:S(2)}) async-start(bf16[8,256,128]{2,1,0:T(8,128)(2,1)} %get-tuple-element.9), calls=%async_computation.1 | async-start | bytes 1048576 | tf_op jit(solution)/shard_map/all_to_all | solution.py:189
where the time goes:
time: 81 us; the launch traced here: 80.4 us
  waiting for transfers between devices  31.3 us (39%)
  Pallas kernels  15.5 us (19%)
  blocking collectives  11.4 us (14%)
  starting transfers between devices  10.9 us (13%)
  local copies, waits for them, and re-layouts  7.08 us (9%)
  other arithmetic  3.44 us (4%)
    all_to_all x1, waiting for transfers between devices, shards_dense(): got = lax.all_to_all(sent, 'ctx', split_axis=0, concat_axis=0, tiled=True)  17.9 us
    all_to_all x1, waiting for transfers between devices, shards_dense(): back = lax.all_to_all(corr, 'ctx', split_axis=0, concat_axis=0, tiled=True)  13.5 us
    all_to_all x1, blocking collectives, shards_dense(): terms = lax.all_to_all(grad, 'dp', split_axis=0, concat_axis=0, tiled=True)  11.4 us
    all_to_all x1, starting transfers between devices, shards_dense(): got = lax.all_to_all(sent, 'ctx', split_axis=0, concat_axis=0, tiled=True)  7.31 us
    unnamed x20, local copies, waits for them, and re-layouts  7.08 us
    pallas_call x1, Pallas kernels, product(): pl.pallas_call(product_kernel, grid=(groups,), in_specs=[spec] * 4, out_s...  5.54 us
    pallas_call x1, Pallas kernels, correlate_dense(): pl.pallas_call(correlate_kernel, in_specs=[vmem] * 3, out_specs=[vmem] *...  5.43 us
    pallas_call x1, Pallas kernels, filter_spectrum_dense(): pl.pallas_call(filter_kernel, grid=(tiles,), in_specs=[pl.BlockSpec((chan...  4.56 us
  transfers between devices with their start and end apart: 2, of which 2 were waited for; matrix products, arithmetic and copies ran while one was open for 1% of the time, Pallas kernels for 6%

commit v1 on v0

--- a/solution.py
+++ b/solution.py
@@ -1,3 +1,4 @@
+import functools
 import math
 
 import jax
@@ -8,11 +9,13 @@
 from jax.experimental.pallas import tpu as pltpu
 from jax.sharding import PartitionSpec as P
 
+
 highest = lax.Precision.HIGHEST
 f32 = jnp.float32
 bf16 = jnp.bfloat16
 LANES = 128
 STEP = 32
+VMEM_LIMIT = 16 * 2**20
 
 
 def tables(length):
@@ -24,26 +27,57 @@
     return pack(hi), pack(lo)
 
 
-def product_kernel(go_ref, po_ref, pr_ref, vb_ref, out_ref):
-    out_ref[0, 0] = (go_ref[0].astype(f32) * po_ref[0].astype(f32)).astype(bf16)
-    out_ref[0, 1] = (pr_ref[0].astype(f32) * vb_ref[0].astype(f32)).astype(bf16)
-
-
-def product(grad_output, post_gate, pre_gate, value_branch, groups):
-    _, channels, block = grad_output.shape
-    rows = channels // groups
-    spec = pl.BlockSpec((1, rows, block), lambda i: (0, i, 0))
+def in_hbm(*arrays):
+    return [pltpu.with_memory_space_constraint(array, pltpu.HBM) for array in arrays]
+
+
+def row_block(axis, offset, count, rows):
+    return pl.ds(pl.multiple_of(lax.rem(lax.axis_index(axis) + offset, count) * rows, rows), rows)
+
+
+def product_kernel(axis, *refs):
+    count = len(refs) - 6
+    in_refs, out_refs = refs[:4], refs[4 : 4 + count]
+    buf_ref, sems = refs[4 + count :]
+    rows = out_refs[0].shape[1]
+    copies = []
+    for k in range(count):
+        block = row_block(axis, k, count, rows)
+        copies.append(
+            [
+                pltpu.make_async_copy(in_ref.at[block], buf_ref.at[j, k], sems.at[j, k])
+                for j, in_ref in enumerate(in_refs)
+            ]
+        )
+        for copy in copies[k]:
+            copy.start()
+    for k, out_ref in enumerate(out_refs):
+        for copy in copies[k]:
+            copy.wait()
+        for j in range(2):
+            left = buf_ref[2 * j, k].astype(f32)
+            out_ref[j] = (left * buf_ref[2 * j + 1, k].astype(f32)).astype(bf16)
+
+
+def product(grad_output, post_gate, pre_gate, value_branch, axis):
+    count = lax.axis_size(axis)
+    channels, block = grad_output.shape
+    rows = channels // count
     return pl.pallas_call(
-        product_kernel,
-        grid=(groups,),
-        in_specs=[spec] * 4,
-        out_specs=pl.BlockSpec((1, 2, rows, block), lambda i: (i, 0, 0, 0)),
-        out_shape=jax.ShapeDtypeStruct((groups, 2, rows, block), bf16),
+        functools.partial(product_kernel, axis),
+        in_specs=[pl.BlockSpec(memory_space=pltpu.HBM)] * 4,
+        out_specs=[pl.BlockSpec(memory_space=pltpu.VMEM)] * count,
+        out_shape=[jax.ShapeDtypeStruct((2, rows, block), bf16)] * count,
+        scratch_shapes=[
+            pltpu.VMEM((4, count, rows, block), bf16),
+            pltpu.SemaphoreType.DMA((4, count)),
+        ],
+        compiler_params=pltpu.CompilerParams(vmem_limit_bytes=4 * 2**20),
         cost_estimate=pl.CostEstimate(
             flops=2 * channels * block, bytes_accessed=12 * channels * block, transcendentals=0
         ),
         name="product",
-    )(grad_output, post_gate, pre_gate, value_branch)
+    )(*in_hbm(grad_output, post_gate, pre_gate, value_branch))
 
 
 def filter_kernel(filt_ref, hi_ref, lo_ref, w_ref, spec_ref):
@@ -95,106 +129,199 @@
             transcendentals=0,
         ),
         name="filter_spectrum",
-    )(filt, jnp.asarray(hi), jnp.asarray(lo))
-
-
-def correlate_kernel(got_ref, w_ref, spec_ref, corr_ref, grad_ref, rows_ref, prod_ref):
-    groups, _, channels, block = got_ref.shape
-    length = groups * block
-    for p in range(groups):
-        cols = pl.ds(p * block, block)
-        rows_ref[:channels, cols] = got_ref[p, 0]
-        rows_ref[channels:, cols] = got_ref[p, 1]
-    lane = lax.broadcasted_iota(jnp.int32, (channels, LANES), 1)
+    )(*in_hbm(filt, jnp.asarray(hi), jnp.asarray(lo)))
+
+
+def multiply_spectra(a_re, a_im, b_re, b_im, first_tile, length):
+    rr = a_re * b_re
+    ii = a_im * b_im
+    cross = a_im * b_re - a_re * b_im
+    if not first_tile:
+        return (rr + ii) * (1.0 / length), cross * (1.0 / length)
+    first = lax.broadcasted_iota(jnp.int32, rr.shape, 1) == 0
+    scale = jnp.where(first, 0.5 / length, 1.0 / length)
+    return jnp.where(first, rr, rr + ii) * scale, jnp.where(first, ii, cross) * scale
+
+
+def inverse(prod_ref, w_ref, taps):
+    return lax.dot_general(
+        prod_ref[...], w_ref[taps, :], (((1,), (1,)), ((), ())), preferred_element_type=f32
+    ).astype(bf16)
+
+
+def correlate_kernel(axis, w_ref, spec_ref, *refs):
+    count = (len(refs) - 3) // 2
+    got_refs, out_refs = refs[:count], refs[count : 2 * count]
+    terms_ref, rows_ref, prod_ref = refs[2 * count :]
+    _, channels, block = got_refs[0].shape
+    length = count * block
+    me = lax.axis_index(axis)
+    for k, got_ref in enumerate(got_refs):
+        rows_ref[lax.rem(me + count - k, count)] = got_ref[...]
+    rows = jnp.concatenate(
+        [rows_ref[p].reshape(2 * channels, block) for p in range(count)], axis=1
+    )
     for n in range(length // LANES):
         re = pl.ds(2 * n * LANES, LANES)
         im = pl.ds((2 * n + 1) * LANES, LANES)
         both = pl.ds(2 * n * LANES, 2 * LANES)
-        spectrum = jnp.dot(rows_ref[...], w_ref[:, both], preferred_element_type=f32)
+        spectrum = jnp.dot(rows, w_ref[:, both], preferred_element_type=f32)
         g_re = spectrum[:channels, :LANES]
         g_im = spectrum[:channels, LANES:]
-        s_re = spectrum[channels:, :LANES]
-        s_im = spectrum[channels:, LANES:]
-        h_re = spec_ref[:, re]
-        h_im = spec_ref[:, im]
-        for y_re, y_im, at in ((h_re, h_im, 0), (s_re, s_im, channels)):
-            rr = g_re * y_re
-            ii = g_im * y_im
-            cross = g_im * y_re - g_re * y_im
-            scale = 1.0 / length
-            if n == 0:
-                first = lane == 0
-                real = jnp.where(first, rr, rr + ii)
-                imag = jnp.where(first, ii, cross)
-                scale = jnp.where(first, 0.5 / length, 1.0 / length)
-            else:
-                real = rr + ii
-                imag = cross
-            out = pl.ds(at, channels)
-            prod_ref[out, re] = (real * scale).astype(bf16)
-            prod_ref[out, im] = (imag * scale).astype(bf16)
-    taps = grad_ref.shape[2]
-    tile = 2 * LANES
-    for q in range(length // tile):
-        out = lax.dot_general(
-            prod_ref[...],
-            w_ref[pl.ds(q * tile, tile), :],
-            (((1,), (1,)), ((), ())),
-            preferred_element_type=f32,
-        )
-        for part in range(tile // block):
-            corr_ref[q * (tile // block) + part] = out[
-                :channels, part * block : (part + 1) * block
-            ].astype(bf16)
-        start = q * tile
-        grad_ref[start // taps, :, pl.ds(start % taps, tile)] = out[channels:].astype(bf16)
-
-
-def correlate_dense(got, w, spec, shares):
-    groups, _, channels, block = got.shape
-    length = groups * block
+        for y_re, y_im, out_ref in (
+            (spec_ref[:, re], spec_ref[:, im], prod_ref),
+            (spectrum[channels:, :LANES], spectrum[channels:, LANES:], terms_ref),
+        ):
+            real, imag = multiply_spectra(g_re, g_im, y_re, y_im, n == 0, length)
+            out_ref[:, re] = real.astype(bf16)
+            out_ref[:, im] = imag.astype(bf16)
+    pair = 2 * LANES // block
+    for q in range(count // pair):
+        out = inverse(prod_ref, w_ref, pl.ds(q * 2 * LANES, 2 * LANES))
+        for part in range(pair):
+            rows_ref[q * pair + part, 0] = out[:, part * block : (part + 1) * block]
+    for k, out_ref in enumerate(out_refs):
+        out_ref[...] = rows_ref[lax.rem(me + k, count), 0]
+
+
+def correlate_dense(got, w, spec, axis):
+    count = len(got)
+    _, channels, block = got[0].shape
+    length = count * block
+    vmem = pl.BlockSpec(memory_space=pltpu.VMEM)
+    *corr, terms = pl.pallas_call(
+        functools.partial(correlate_kernel, axis),
+        in_specs=[vmem] * (2 + count),
+        out_specs=[vmem] * (count + 1),
+        out_shape=[jax.ShapeDtypeStruct((channels, block), bf16)] * count
+        + [jax.ShapeDtypeStruct((channels, 2 * length), bf16)],
+        scratch_shapes=[
+            pltpu.VMEM((count, 2, channels, block), bf16),
+            pltpu.VMEM((channels, 2 * length), bf16),
+        ],
+        compiler_params=pltpu.CompilerParams(vmem_limit_bytes=VMEM_LIMIT),
+        cost_estimate=pl.CostEstimate(
+            flops=12 * channels * length * length,
+            bytes_accessed=4 * length * length + 20 * channels * length,
+            transcendentals=0,
+        ),
+        name="correlate",
+    )(w, spec, *got)
+    return corr, terms
+
+
+def gradient_kernel(axis, w_ref, terms_ref, *out_refs):
+    shares = len(out_refs)
+    taps = out_refs[0].shape[1]
+    for k, out_ref in enumerate(out_refs):
+        out_ref[...] = inverse(terms_ref, w_ref, row_block(axis, k, shares, taps))
+
+
+def gradient_dense(terms, w, axis):
+    shares = lax.axis_size(axis)
+    channels = terms.shape[0]
+    length = terms.shape[1] // 2
     vmem = pl.BlockSpec(memory_space=pltpu.VMEM)
     return pl.pallas_call(
-        correlate_kernel,
-        in_specs=[vmem] * 3,
-        out_specs=[vmem] * 2,
-        out_shape=[
-            jax.ShapeDtypeStruct((groups, channels, block), bf16),
-            jax.ShapeDtypeStruct((shares, channels, length // shares), bf16),
-        ],
+        functools.partial(gradient_kernel, axis),
+        in_specs=[vmem] * 2,
+        out_specs=[vmem] * shares,
+        out_shape=[jax.ShapeDtypeStruct((channels, length // shares), bf16)] * shares,
+        compiler_params=pltpu.CompilerParams(vmem_limit_bytes=VMEM_LIMIT),
+        cost_estimate=pl.CostEstimate(
+            flops=4 * channels * length * length,
+            bytes_accessed=4 * length * length + 6 * channels * length,
+            transcendentals=0,
+        ),
+        name="gradient",
+    )(w, terms)
+
+
+def finish_kernel(axis, shares, scale, base_ref, pr_ref, vb_ref, *refs):
+    count = len(refs) - shares - 7
+    back_refs, term_refs = refs[:count], refs[count : count + shares]
+    pre_out, value_out, grad_out, pre_buf, value_buf, grad_buf, sems = refs[count + shares :]
+    rows = back_refs[0].shape[0]
+    copies = []
+
+    def send(source, target, sem):
+        copy = pltpu.make_async_copy(source, target, sem)
+        copy.start()
+        copies.append(copy)
+
+    for k, back_ref in enumerate(back_refs):
+        block = row_block(axis, count - k, count, rows)
+        summed = back_ref[...].astype(f32) + base_ref[block]
+        pre_buf[k] = (summed * vb_ref[block].astype(f32)).astype(bf16)
+        value_buf[k] = (summed * pr_ref[block].astype(f32)).astype(bf16)
+        send(pre_buf.at[k], pre_out.at[block], sems.at[0, k])
+        send(value_buf.at[k], value_out.at[block], sems.at[1, k])
+    grad_buf[...] = sum(term_ref[...].astype(f32) for term_ref in term_refs) * scale
+    send(grad_buf, grad_out, sems.at[2, 0])
+    for copy in copies:
+        copy.wait()
+
+
+def finish(back, base, pre_gate, value_branch, terms, scale, axis):
+    count = len(back)
+    shares = len(terms)
+    rows, block = back[0].shape
+    channels = count * rows
+    vmem = pl.BlockSpec(memory_space=pltpu.VMEM)
+    return pl.pallas_call(
+        functools.partial(finish_kernel, axis, shares, scale),
+        in_specs=[vmem] * (3 + count + shares),
+        out_specs=[pl.BlockSpec(memory_space=pltpu.HBM)] * 3,
+        out_shape=[jax.ShapeDtypeStruct((channels, block), bf16)] * 2
+        + [jax.ShapeDtypeStruct(terms[0].shape, f32)],
         scratch_shapes=[
-            pltpu.VMEM((2 * channels, length), bf16),
-            pltpu.VMEM((2 * channels, 2 * length), bf16),
-        ],
-        compiler_params=pltpu.CompilerParams(vmem_limit_bytes=32 * 2**20),
+            pltpu.VMEM((count, rows, block), bf16),
+            pltpu.VMEM((count, rows, block), bf16),
+            pltpu.VMEM(terms[0].shape, f32),
+            pltpu.SemaphoreType.DMA((3, count)),
+        ],
+        compiler_params=pltpu.CompilerParams(vmem_limit_bytes=8 * 2**20),
         cost_estimate=pl.CostEstimate(
-            flops=16 * channels * length * length,
-            bytes_accessed=4 * length * length + 20 * channels * length,
-            transcendentals=0,
-        ),
-        name="correlate",
-    )(got, w, spec)
+            flops=3 * channels * block, bytes_accessed=14 * channels * block, transcendentals=0
+        ),
+        name="finish",
+    )(base, pre_gate, value_branch, *back, *terms)
+
+
+def ahead(value, axis, k):
+    count = lax.axis_size(axis)
+    return lax.ppermute(value, axis, [(j, (j + k) % count) for j in range(count)])
+
+
+def exchange(blocks, axis):
+    got = [blocks[0]]
+    for k in range(1, len(blocks)):
+        got.append(ahead(blocks[k], axis, k))
+    return got
 
 
 def shards_dense(grad_output, post_gate, pre_gate, value_branch, long_filter, skip_weight):
-    groups = lax.axis_size("ctx")
     shares = lax.axis_size("dp")
     seqs, channels, block = grad_output.shape
     length = long_filter.shape[1]
     token_count = seqs * shares * length
-    sent = product(grad_output, post_gate, pre_gate, value_branch, groups)
+    grad_rows, post_rows, pre_rows, value_rows = (
+        x.reshape(channels, block) for x in (grad_output, post_gate, pre_gate, value_branch)
+    )
+    sent = product(grad_rows, post_rows, pre_rows, value_rows, "ctx")
+    got = exchange(sent, "ctx")
     w, spec = filter_spectrum_dense(long_filter)
-    got = lax.all_to_all(sent, "ctx", split_axis=0, concat_axis=0, tiled=True)
-    corr, grad = correlate_dense(got, w, spec, shares)
-    back = lax.all_to_all(corr, "ctx", split_axis=0, concat_axis=0, tiled=True)
-    terms = lax.all_to_all(grad, "dp", split_axis=0, concat_axis=0, tiled=True)
-    returned = back.reshape(seqs, channels, block)
-    gated = (grad_output.astype(f32) * post_gate.astype(f32)).astype(bf16)
-    summed = returned.astype(f32) + skip_weight[None, :, None] * gated.astype(f32)
-    grad_pre_gate = (summed * value_branch.astype(f32)).astype(bf16)
-    grad_value_branch = (summed * pre_gate.astype(f32)).astype(bf16)
-    grad_long_filter = jnp.sum(terms.astype(f32), axis=0) * (1.0 / math.sqrt(token_count))
-    return (grad_pre_gate, grad_value_branch, grad_long_filter)
+    gated = (grad_rows.astype(f32) * post_rows.astype(f32)).astype(bf16)
+    base = skip_weight[:, None] * gated.astype(f32)
+    corr, terms = correlate_dense(got, w, spec, "ctx")
+    back = exchange(corr, "ctx")
+    terms = gradient_dense(terms, w, "dp")
+    terms = exchange(terms, "dp")
+    grad_pre_gate, grad_value_branch, grad_long_filter = finish(
+        back, base, pre_rows, value_rows, terms, 1.0 / math.sqrt(token_count), "ctx"
+    )
+    shape = grad_output.shape
+    return (grad_pre_gate.reshape(shape), grad_value_branch.reshape(shape), grad_long_filter)
 
 
 def split_factor(length):

time: 81 us -> 59.3 us (0.73)
  starting transfers between devices: 10.9 us -> 34 us
  waiting for transfers between devices: 31.3 us -> 8.97 us
  blocking collectives: 11.4 us -> 0 us
  local copies, waits for them, and re-layouts: 7.08 us -> 0.03 us
  other arithmetic: 3.44 us -> 0.35 us
    ppermute x0 -> x17, starting transfers between devices: none -> 34 us  [ahead(): lax.ppermute(value, axis, [(j, (j + k) % count) for j in range(count)])]
    all_to_all x2 -> x0, waiting for transfers between devices: 31.3 us -> none  [the longest x1 17.9 us: shards_dense(): got = lax.all_to_all(sent, 'ctx', split_axis=0, concat_axis=0, tiled=True)]
    all_to_all x1 -> x0, blocking collectives: 11.4 us -> none  [shards_dense(): terms = lax.all_to_all(grad, 'dp', split_axis=0, concat_axis=0, tiled=True)]
    all_to_all x2 -> x0, starting transfers between devices: 10.9 us -> none  [the longest x1 7.31 us: shards_dense(): got = lax.all_to_all(sent, 'ctx', split_axis=0, concat_axis=0, tiled=True)]
    ppermute x0 -> x17, waiting for transfers between devices: none -> 8.97 us  [ahead(): lax.ppermute(value, axis, [(j, (j + k) % count) for j in range(count)])]
    unnamed x20 -> x10, local copies, waits for them, and re-layouts: 7.08 us -> 0.03 us
    pallas_call x2 -> x4, Pallas kernels: 11 us -> 8.23 us  [the longest x1 3.78 us: correlate_dense(): pl.pallas_call(functools.partial(correlate_kernel, axis), in_specs=[vmem]...]
    convert_element_type x1 -> x0, other arithmetic: 2.65 us -> none  [shards_dense(): grad_value_branch = (summed * pre_gate.astype(f32)).astype(bf16)]
  transfers between devices with their start and end apart: 2 -> 17, of which waited for: 2 -> 5; matrix products, arithmetic and copies ran while one was open for 1% -> 1% of each run, Pallas kernels for 6% -> 13%
where the time goes in v1:
time: 59.3 us; the launch traced here: 58.8 us
  starting transfers between devices  34 us (57%)
  Pallas kernels  14.7 us (25%)
  waiting for transfers between devices  8.97 us (15%)
  between operations  0.78 us (1%)
    ppermute x17, starting transfers between devices, ahead(): lax.ppermute(value, axis, [(j, (j + k) % count) for j in range(count)])  34 us
    ppermute x17, waiting for transfers between devices, ahead(): lax.ppermute(value, axis, [(j, (j + k) % count) for j in range(count)])  8.97 us
    pallas_call x1, Pallas kernels, filter_spectrum_dense(): pl.pallas_call(filter_kernel, grid=(tiles,), in_specs=[pl.BlockSpec((chan...  6.42 us
    pallas_call x1, Pallas kernels, correlate_dense(): pl.pallas_call(functools.partial(correlate_kernel, axis), in_specs=[vmem]...  3.78 us
    pallas_call x1, Pallas kernels, product(): pl.pallas_call(functools.partial(product_kernel, axis), in_specs=[pl.Bloc...  1.89 us
    pallas_call x1, Pallas kernels, finish(): pl.pallas_call(functools.partial(finish_kernel, axis, shares, scale), in_...  1.29 us
    pallas_call x1, Pallas kernels, gradient_dense(): pl.pallas_call(functools.partial(gradient_kernel, axis), in_specs=[vmem]...  1.28 us
  transfers between devices with their start and end apart: 17, of which 5 were waited for; matrix products, arithmetic and copies ran while one was open for 1% of the time, Pallas kernels for 13%

profile of v1, /device:TPU:0, one launch (start us, length us, event | category | flops | bytes accessed | tf_op | source)
XLA Modules:
  0.0 58.8 jit_solution(13526220661911580551)
XLA Ops:
  0.6 1.9 %product.1 = (bf16[2,256,128]{2,1,0:T(8,128)(2,1)S(1)}, bf16[2,256,128]{2,1,0:T(8,128)(2,1)S(1)}, bf16[2,256,128]{2,1,0:T(8,128)(2,1)S(1)}, bf16[2,256,128]{2,1,...) custom-call(bf16[2048,128]{1,0:T(8,128)(2,1)} %bitcast.13, ...), custom_call_target="tpu_custom_call" | custom-call | flops 524288 | bytes 3145728 | tf_op jit(solution)/shard_map/product/pallas_call | solution.py:66
  2.5 3.0 %collective-permute-start = (bf16[2,256,128]{2,1,0:T(8,128)(2,1)S(1)}, bf16[2,256,128]{2,1,0:T(8,128)(2,1)S(1)}, u32[]{:S(2)}, u32[]{:S(2)}) collective-permute-start(bf16[2,256,128]{2,1,0:T(8,128)(2,1)S(1)} %get-tuple-element.32), channel_id=1, source_target_pairs={{0,1},{1,2},{2,3},{3,4},{4,5},{5,6},{6,7},{7,0},{8,9},{9,10},{10,1... | collective-permute-start | bytes 393224 | tf_op jit(solution)/shard_map/ppermute | solution.py:293
  5.6 1.6 %collective-permute-start.1 = (bf16[2,256,128]{2,1,0:T(8,128)(2,1)S(1)}, bf16[2,256,128]{2,1,0:T(8,128)(2,1)S(1)}, u32[]{:S(2)}, u32[]{:S(2)}) collective-permute-start(bf16[2,256,128]{2,1,0:T(8,128)(2,1)S(1)} %get-tuple-element.33), channel_id=1, source_target_pairs={{0,2},{1,3},{2,4},{3,5},{4,6},{5,7},{6,0},{7,1},{8,10},{9,11},{10,... | collective-permute-start | bytes 393224 | tf_op jit(solution)/shard_map/ppermute | solution.py:293
  7.1 2.5 %collective-permute-start.2 = (bf16[2,256,128]{2,1,0:T(8,128)(2,1)S(1)}, bf16[2,256,128]{2,1,0:T(8,128)(2,1)S(1)}, u32[]{:S(2)}, u32[]{:S(2)}) collective-permute-start(bf16[2,256,128]{2,1,0:T(8,128)(2,1)S(1)} %get-tuple-element.34), channel_id=1, source_target_pairs={{0,3},{1,4},{2,5},{3,6},{4,7},{5,0},{6,1},{7,2},{8,11},{9,12},{10,... | collective-permute-start | bytes 393224 | tf_op jit(solution)/shard_map/ppermute | solution.py:293
  9.7 1.2 %collective-permute-start.3 = (bf16[2,256,128]{2,1,0:T(8,128)(2,1)S(1)}, bf16[2,256,128]{2,1,0:T(8,128)(2,1)S(1)}, u32[]{:S(2)}, u32[]{:S(2)}) collective-permute-start(bf16[2,256,128]{2,1,0:T(8,128)(2,1)S(1)} %get-tuple-element.35), channel_id=1, source_target_pairs={{0,4},{1,5},{2,6},{3,7},{4,0},{5,1},{6,2},{7,3},{8,12},{9,13},{10,... | collective-permute-start | bytes 393224 | tf_op jit(solution)/shard_map/ppermute | solution.py:293
  10.9 2.6 %collective-permute-start.4 = (bf16[2,256,128]{2,1,0:T(8,128)(2,1)S(1)}, bf16[2,256,128]{2,1,0:T(8,128)(2,1)S(1)}, u32[]{:S(2)}, u32[]{:S(2)}) collective-permute-start(bf16[2,256,128]{2,1,0:T(8,128)(2,1)S(1)} %get-tuple-element.36), channel_id=1, source_target_pairs={{0,5},{1,6},{2,7},{3,0},{4,1},{5,2},{6,3},{7,4},{8,13},{9,14},{10,... | collective-permute-start | bytes 393224 | tf_op jit(solution)/shard_map/ppermute | solution.py:293
  13.6 0.0 collective-permute-done.refs_1_
  13.6 1.4 %collective-permute-start.5 = (bf16[2,256,128]{2,1,0:T(8,128)(2,1)S(1)}, bf16[2,256,128]{2,1,0:T(8,128)(2,1)S(1)}, u32[]{:S(2)}, u32[]{:S(2)}) collective-permute-start(bf16[2,256,128]{2,1,0:T(8,128)(2,1)S(1)} %get-tuple-element.37), channel_id=1, source_target_pairs={{0,6},{1,7},{2,0},{3,1},{4,2},{5,3},{6,4},{7,5},{8,14},{9,15},{10,... | collective-permute-start | bytes 393224 | tf_op jit(solution)/shard_map/ppermute | solution.py:293
  14.9 0.0 collective-permute-done.1.refs_2_
  14.9 2.1 %collective-permute-start.6 = (bf16[2,256,128]{2,1,0:T(8,128)(2,1)S(1)}, bf16[2,256,128]{2,1,0:T(8,128)(2,1)S(1)}, u32[]{:S(2)}, u32[]{:S(2)}) collective-permute-start(bf16[2,256,128]{2,1,0:T(8,128)(2,1)S(1)} %get-tuple-element.38), channel_id=1, source_target_pairs={{0,7},{1,0},{2,1},{3,2},{4,3},{5,4},{6,5},{7,6},{8,15},{9,8},{10,9... | collective-permute-start | bytes 393224 | tf_op jit(solution)/shard_map/ppermute | solution.py:293
  17.0 6.4 %filter_spectrum.1 = (bf16[1024,2048]{1,0:T(8,128)(2,1)S(1)}, f32[256,2048]{1,0:T(8,128)S(1)}) custom-call(f32[256,1024]{1,0:T(8,128)} %filt_ref.1, f32[2,32,1024]{2,1,0:T(8,128)} %constant.4.clone.hi_ref, f32[2,32,1024]{2,1,0:T(8,128)} %constant.5.clone.lo_ref), custom_call_target="tpu_custom_call" | custom-call | flops 1073741824 | bytes 7340032 | tf_op jit(solution)/shard_map/filter_spectrum/pallas_call | solution.py:109
  23.4 0.1 collective-permute-done.2.refs_3_
  23.5 0.3 collective-permute-done.3.refs_4_
  23.8 0.0 collective-permute-done.4.refs_5_
  23.8 0.0 collective-permute-done.5.refs_6_
  23.8 0.0 collective-permute-done.6.refs_7_
  23.8 3.8 %correlate.1 = (bf16[256,128]{1,0:T(8,128)(2,1)S(1)}, bf16[256,128]{1,0:T(8,128)(2,1)S(1)}, bf16[256,128]{1,0:T(8,128)(2,1)S(1)}, bf16[256,128]{1,0:T(8,128)(2,1...) custom-call(bf16[1024,2048]{1,0:T(8,128)(2,1)S(1)} %get-tuple-elemen, ...), custom_call_target="tpu_custom_call" | custom-call | flops 3221225472 | bytes 9437184 | tf_op jit(solution)/shard_map/correlate/pallas_call | solution.py:192
  27.6 0.0 copy-start.2
  27.6 0.0 copy-start.3
  27.6 0.0 copy-start.4
  27.6 0.0 copy-start
  27.7 0.0 copy-start.1
  27.7 10.2 %collective-permute-start.10 = (bf16[256,128]{1,0:T(8,128)(2,1)S(1)}, bf16[256,128]{1,0:T(8,128)(2,1)S(1)}, u32[]{:S(2)}, u32[]{:S(2)}) collective-permute-start(bf16[256,128]{1,0:T(8,128)(2,1)S(1)} %get-tuple-element.43), channel_id=1, source_target_pairs={{0,4},{1,5},{2,6},{3,7},{4,0},{5,1},{6,2},{7,3},{8,12},{9,13},{10,... | collective-permute-start | bytes 196616 | tf_op jit(solution)/shard_map/ppermute | solution.py:293
  37.9 0.5 collective-permute-start.11
  38.4 3.0 %collective-permute-start.12 = (bf16[256,128]{1,0:T(8,128)(2,1)S(1)}, bf16[256,128]{1,0:T(8,128)(2,1)S(1)}, u32[]{:S(2)}, u32[]{:S(2)}) collective-permute-start(bf16[256,128]{1,0:T(8,128)(2,1)S(1)} %get-tuple-element.45), channel_id=1, source_target_pairs={{0,6},{1,7},{2,0},{3,1},{4,2},{5,3},{6,4},{7,5},{8,14},{9,15},{10,... | collective-permute-start | bytes 196616 | tf_op jit(solution)/shard_map/ppermute | solution.py:293
  41.4 2.8 %collective-permute-start.13 = (bf16[256,128]{1,0:T(8,128)(2,1)S(1)}, bf16[256,128]{1,0:T(8,128)(2,1)S(1)}, u32[]{:S(2)}, u32[]{:S(2)}) collective-permute-start(bf16[256,128]{1,0:T(8,128)(2,1)S(1)} %get-tuple-element.46), channel_id=1, source_target_pairs={{0,7},{1,0},{2,1},{3,2},{4,3},{5,4},{6,5},{7,6},{8,15},{9,8},{10,9... | collective-permute-start | bytes 196616 | tf_op jit(solution)/shard_map/ppermute | solution.py:293
  44.2 0.0 collective-permute-start.7
  44.2 1.3 %gradient.1 = (bf16[256,256]{1,0:T(8,128)(2,1)S(1)}, bf16[256,256]{1,0:T(8,128)(2,1)S(1)}, bf16[256,256]{1,0:T(8,128)(2,1)S(1)}, bf16[256,256]{1,0:T(8,128)(2,1)S(1)}) custom-call(bf16[1024,2048]{1,0:T(8,128)(2,1)S(1)} %get-tuple-element.29.w_ref, bf16[256,2048]{1,0:T(8,128)(2,1)S(1)} %get-tuple-element.47.terms_ref), custom_call_target="tpu_custom_call" | custom-call | flops 1073741824 | bytes 5767168 | tf_op jit(solution)/shard_map/gradient/pallas_call | solution.py:225
  45.5 0.0 collective-permute-done.10.refs_4_
  45.5 0.1 collective-permute-start.14
  45.6 0.0 collective-permute-done.11.refs_5_
  45.6 1.6 %collective-permute-start.15 = (bf16[256,256]{1,0:T(8,128)(2,1)S(1)}, bf16[256,256]{1,0:T(8,128)(2,1)S(1)}, u32[]{:S(2)}, u32[]{:S(2)}) collective-permute-start(bf16[256,256]{1,0:T(8,128)(2,1)S(1)} %get-tuple-element.50), channel_id=1, source_target_pairs={{0,16},{8,24},{16,0},{24,8},{1,17},{9,25},{17,1},{25,9},{2,18},{10... | collective-permute-start | bytes 393224 | tf_op jit(solution)/shard_map/ppermute | solution.py:293
  47.1 0.0 collective-permute-done.12.refs_6_
  47.1 1.4 %collective-permute-start.16 = (bf16[256,256]{1,0:T(8,128)(2,1)S(1)}, bf16[256,256]{1,0:T(8,128)(2,1)S(1)}, u32[]{:S(2)}, u32[]{:S(2)}) collective-permute-start(bf16[256,256]{1,0:T(8,128)(2,1)S(1)} %get-tuple-element.51), channel_id=1, source_target_pairs={{0,24},{8,0},{16,8},{24,16},{1,25},{9,1},{17,9},{25,17},{2,26},{10... | collective-permute-start | bytes 393224 | tf_op jit(solution)/shard_map/ppermute | solution.py:293
  48.5 0.0 collective-permute-done.13.refs_7_
  48.5 0.0 collective-permute-start.8
  48.5 2.6 %collective-permute-done.7.refs_1_ = bf16[256,128]{1,0:T(8,128)(2,1)S(1)} collective-permute-done((bf16[256,128]{1,0:T(8,128)(2,1)S(1)}, bf16[256,128]{1,0:T(8,128)(2,1)S(1)}, u32[]{:S(2)}, u32[]{:S(2)}) %collective-permute-start.7) | collective-permute-done | bytes 65568 | tf_op jit(solution)/shard_map/ppermute | solution.py:293
  51.2 0.0 collective-permute-start.9
  51.2 0.0 copy-done.2
  51.2 0.0 copy-done.3
  51.2 0.0 copy-done.4
  51.2 0.3 convert_multiply_fusion.base_ref
  51.5 3.2 %collective-permute-done.8.refs_2_ = bf16[256,128]{1,0:T(8,128)(2,1)S(1)} collective-permute-done((bf16[256,128]{1,0:T(8,128)(2,1)S(1)}, bf16[256,128]{1,0:T(8,128)(2,1)S(1)}, u32[]{:S(2)}, u32[]{:S(2)}) %collective-permute-start.8) | collective-permute-done | bytes 65568 | tf_op jit(solution)/shard_map/ppermute | solution.py:293
  54.7 2.7 %collective-permute-done.9.refs_3_ = bf16[256,128]{1,0:T(8,128)(2,1)S(1)} collective-permute-done((bf16[256,128]{1,0:T(8,128)(2,1)S(1)}, bf16[256,128]{1,0:T(8,128)(2,1)S(1)}, u32[]{:S(2)}, u32[]{:S(2)}) %collective-permute-start.9) | collective-permute-done | bytes 65568 | tf_op jit(solution)/shard_map/ppermute | solution.py:293
  57.4 0.0 collective-permute-done.14.refs_9_
  57.4 0.0 collective-permute-done.15.refs_10_
  57.4 0.0 collective-permute-done.16.refs_11_
  57.5 1.3 %finish.1 = (bf16[2048,128]{1,0:T(8,128)(2,1)}, bf16[2048,128]{1,0:T(8,128)(2,1)}, f32[256,256]{1,0:T(8,128)}) custom-call(f32[2048,128]{1,0:T(8,128)S(1)} %convert_multiply_fusion.base_ref, bf16[2048,128]{1,0:T(8,128)(2,1)S(1)} %bitcast.9, bf16[2048,128]{1,0:T(8,128)(2,1)S(1)} %bitcast.11, bf16[256,128]{1,0:T(8,128)(2,1)S(1)} %get-tuple-element.39.refs_0_, ...), custom_call_target="tpu_custom_call" | custom-call | flops 786432 | bytes 3670016 | tf_op jit(solution)/shard_map/finish/pallas_call | solution.py:271
  (2 shorter events, 0.0 us)
Async XLA Ops:
  2.5 11.0 %collective-permute-start = (bf16[2,256,128]{2,1,0:T(8,128)(2,1)S(1)}, bf16[2,256,128]{2,1,0:T(8,128)(2,1)S(1)}, u32[]{:S(2)}, u32[]{:S(2)}) collective-permute-start(bf16[2,256,128]{2,1,0:T(8,128)(2,1)S(1)} %get-tuple-element.32), channel_id=1, source_target_pairs={{0,1},{1,2},{2,3},{3,4},{4,5},{5,6},{6,7},{7,0},{8,9},{9,10},{10,1... | collective-permute-start | bytes 393224 | tf_op jit(solution)/shard_map/ppermute | solution.py:293
  5.6 9.4 %collective-permute-start.1 = (bf16[2,256,128]{2,1,0:T(8,128)(2,1)S(1)}, bf16[2,256,128]{2,1,0:T(8,128)(2,1)S(1)}, u32[]{:S(2)}, u32[]{:S(2)}) collective-permute-start(bf16[2,256,128]{2,1,0:T(8,128)(2,1)S(1)} %get-tuple-element.33), channel_id=1, source_target_pairs={{0,2},{1,3},{2,4},{3,5},{4,6},{5,7},{6,0},{7,1},{8,10},{9,11},{10,... | collective-permute-start | bytes 393224 | tf_op jit(solution)/shard_map/ppermute | solution.py:293
  7.1 16.3 %collective-permute-start.2 = (bf16[2,256,128]{2,1,0:T(8,128)(2,1)S(1)}, bf16[2,256,128]{2,1,0:T(8,128)(2,1)S(1)}, u32[]{:S(2)}, u32[]{:S(2)}) collective-permute-start(bf16[2,256,128]{2,1,0:T(8,128)(2,1)S(1)} %get-tuple-element.34), channel_id=1, source_target_pairs={{0,3},{1,4},{2,5},{3,6},{4,7},{5,0},{6,1},{7,2},{8,11},{9,12},{10,... | collective-permute-start | bytes 393224 | tf_op jit(solution)/shard_map/ppermute | solution.py:293
  9.7 14.1 %collective-permute-start.3 = (bf16[2,256,128]{2,1,0:T(8,128)(2,1)S(1)}, bf16[2,256,128]{2,1,0:T(8,128)(2,1)S(1)}, u32[]{:S(2)}, u32[]{:S(2)}) collective-permute-start(bf16[2,256,128]{2,1,0:T(8,128)(2,1)S(1)} %get-tuple-element.35), channel_id=1, source_target_pairs={{0,4},{1,5},{2,6},{3,7},{4,0},{5,1},{6,2},{7,3},{8,12},{9,13},{10,... | collective-permute-start | bytes 393224 | tf_op jit(solution)/shard_map/ppermute | solution.py:293
  10.9 12.9 %collective-permute-start.4 = (bf16[2,256,128]{2,1,0:T(8,128)(2,1)S(1)}, bf16[2,256,128]{2,1,0:T(8,128)(2,1)S(1)}, u32[]{:S(2)}, u32[]{:S(2)}) collective-permute-start(bf16[2,256,128]{2,1,0:T(8,128)(2,1)S(1)} %get-tuple-element.36), channel_id=1, source_target_pairs={{0,5},{1,6},{2,7},{3,0},{4,1},{5,2},{6,3},{7,4},{8,13},{9,14},{10,... | collective-permute-start | bytes 393224 | tf_op jit(solution)/shard_map/ppermute | solution.py:293
  13.6 10.3 %collective-permute-start.5 = (bf16[2,256,128]{2,1,0:T(8,128)(2,1)S(1)}, bf16[2,256,128]{2,1,0:T(8,128)(2,1)S(1)}, u32[]{:S(2)}, u32[]{:S(2)}) collective-permute-start(bf16[2,256,128]{2,1,0:T(8,128)(2,1)S(1)} %get-tuple-element.37), channel_id=1, source_target_pairs={{0,6},{1,7},{2,0},{3,1},{4,2},{5,3},{6,4},{7,5},{8,14},{9,15},{10,... | collective-permute-start | bytes 393224 | tf_op jit(solution)/shard_map/ppermute | solution.py:293
  14.9 8.9 %collective-permute-start.6 = (bf16[2,256,128]{2,1,0:T(8,128)(2,1)S(1)}, bf16[2,256,128]{2,1,0:T(8,128)(2,1)S(1)}, u32[]{:S(2)}, u32[]{:S(2)}) collective-permute-start(bf16[2,256,128]{2,1,0:T(8,128)(2,1)S(1)} %get-tuple-element.38), channel_id=1, source_target_pairs={{0,7},{1,0},{2,1},{3,2},{4,3},{5,4},{6,5},{7,6},{8,15},{9,8},{10,9... | collective-permute-start | bytes 393224 | tf_op jit(solution)/shard_map/ppermute | solution.py:293
  27.6 23.6 %copy-start.2 = (bf16[1,2048,128]{2,1,0:T(8,128)(2,1)S(1)}, bf16[1,2048,128]{2,1,0:T(8,128)(2,1)}, u32[]{:S(2)}) copy-start(bf16[1,2048,128]{2,1,0:T(8,128)(2,1)} %param.9) | copy-start | bytes 1572868
  27.6 23.5 %copy-start.3 = (bf16[1,2048,128]{2,1,0:T(8,128)(2,1)S(1)}, bf16[1,2048,128]{2,1,0:T(8,128)(2,1)}, u32[]{:S(2)}) copy-start(bf16[1,2048,128]{2,1,0:T(8,128)(2,1)} %param.8) | copy-start | bytes 1572868
  27.6 23.5 %copy-start.4 = (f32[2048]{0:T(1024)S(1)}, f32[2048]{0:T(1024)}, u32[]{:S(2)}) copy-start(f32[2048]{0:T(1024)} %param.13) | copy-start | bytes 24580
  27.6 29.8 %copy-start = (bf16[1,2048,128]{2,1,0:T(8,128)(2,1)S(1)}, bf16[1,2048,128]{2,1,0:T(8,128)(2,1)}, u32[]{:S(2)}) copy-start(bf16[1,2048,128]{2,1,0:T(8,128)(2,1)} %param.10) | copy-start | bytes 1572868
  27.7 29.8 %copy-start.1 = (bf16[1,2048,128]{2,1,0:T(8,128)(2,1)S(1)}, bf16[1,2048,128]{2,1,0:T(8,128)(2,1)}, u32[]{:S(2)}) copy-start(bf16[1,2048,128]{2,1,0:T(8,128)(2,1)} %param.11) | copy-start | bytes 1572868
  27.7 17.8 %collective-permute-start.10 = (bf16[256,128]{1,0:T(8,128)(2,1)S(1)}, bf16[256,128]{1,0:T(8,128)(2,1)S(1)}, u32[]{:S(2)}, u32[]{:S(2)}) collective-permute-start(bf16[256,128]{1,0:T(8,128)(2,1)S(1)} %get-tuple-element.43), channel_id=1, source_target_pairs={{0,4},{1,5},{2,6},{3,7},{4,0},{5,1},{6,2},{7,3},{8,12},{9,13},{10,... | collective-permute-start | bytes 196616 | tf_op jit(solution)/shard_map/ppermute | solution.py:293
  37.9 7.7 %collective-permute-start.11 = (bf16[256,128]{1,0:T(8,128)(2,1)S(1)}, bf16[256,128]{1,0:T(8,128)(2,1)S(1)}, u32[]{:S(2)}, u32[]{:S(2)}) collective-permute-start(bf16[256,128]{1,0:T(8,128)(2,1)S(1)} %get-tuple-element.44), channel_id=1, source_target_pairs={{0,5},{1,6},{2,7},{3,0},{4,1},{5,2},{6,3},{7,4},{8,13},{9,14},{10,... | collective-permute-start | bytes 196616 | tf_op jit(solution)/shard_map/ppermute | solution.py:293
  38.4 8.7 %collective-permute-start.12 = (bf16[256,128]{1,0:T(8,128)(2,1)S(1)}, bf16[256,128]{1,0:T(8,128)(2,1)S(1)}, u32[]{:S(2)}, u32[]{:S(2)}) collective-permute-start(bf16[256,128]{1,0:T(8,128)(2,1)S(1)} %get-tuple-element.45), channel_id=1, source_target_pairs={{0,6},{1,7},{2,0},{3,1},{4,2},{5,3},{6,4},{7,5},{8,14},{9,15},{10,... | collective-permute-start | bytes 196616 | tf_op jit(solution)/shard_map/ppermute | solution.py:293
  41.4 7.1 %collective-permute-start.13 = (bf16[256,128]{1,0:T(8,128)(2,1)S(1)}, bf16[256,128]{1,0:T(8,128)(2,1)S(1)}, u32[]{:S(2)}, u32[]{:S(2)}) collective-permute-start(bf16[256,128]{1,0:T(8,128)(2,1)S(1)} %get-tuple-element.46), channel_id=1, source_target_pairs={{0,7},{1,0},{2,1},{3,2},{4,3},{5,4},{6,5},{7,6},{8,15},{9,8},{10,9... | collective-permute-start | bytes 196616 | tf_op jit(solution)/shard_map/ppermute | solution.py:293
  44.2 7.0 %collective-permute-start.7 = (bf16[256,128]{1,0:T(8,128)(2,1)S(1)}, bf16[256,128]{1,0:T(8,128)(2,1)S(1)}, u32[]{:S(2)}, u32[]{:S(2)}) collective-permute-start(bf16[256,128]{1,0:T(8,128)(2,1)S(1)} %get-tuple-element.40), channel_id=1, source_target_pairs={{0,1},{1,2},{2,3},{3,4},{4,5},{5,6},{6,7},{7,0},{8,9},{9,10},{10,1... | collective-permute-start | bytes 196616 | tf_op jit(solution)/shard_map/ppermute | solution.py:293
  45.5 11.9 %collective-permute-start.14 = (bf16[256,256]{1,0:T(8,128)(2,1)S(1)}, bf16[256,256]{1,0:T(8,128)(2,1)S(1)}, u32[]{:S(2)}, u32[]{:S(2)}) collective-permute-start(bf16[256,256]{1,0:T(8,128)(2,1)S(1)} %get-tuple-element.49), channel_id=1, source_target_pairs={{0,8},{8,16},{16,24},{24,0},{1,9},{9,17},{17,25},{25,1},{2,10},{10... | collective-permute-start | bytes 393224 | tf_op jit(solution)/shard_map/ppermute | solution.py:293
  45.6 11.9 %collective-permute-start.15 = (bf16[256,256]{1,0:T(8,128)(2,1)S(1)}, bf16[256,256]{1,0:T(8,128)(2,1)S(1)}, u32[]{:S(2)}, u32[]{:S(2)}) collective-permute-start(bf16[256,256]{1,0:T(8,128)(2,1)S(1)} %get-tuple-element.50), channel_id=1, source_target_pairs={{0,16},{8,24},{16,0},{24,8},{1,17},{9,25},{17,1},{25,9},{2,18},{10... | collective-permute-start | bytes 393224 | tf_op jit(solution)/shard_map/ppermute | solution.py:293
  47.1 10.3 %collective-permute-start.16 = (bf16[256,256]{1,0:T(8,128)(2,1)S(1)}, bf16[256,256]{1,0:T(8,128)(2,1)S(1)}, u32[]{:S(2)}, u32[]{:S(2)}) collective-permute-start(bf16[256,256]{1,0:T(8,128)(2,1)S(1)} %get-tuple-element.51), channel_id=1, source_target_pairs={{0,24},{8,0},{16,8},{24,16},{1,25},{9,1},{17,9},{25,17},{2,26},{10... | collective-permute-start | bytes 393224 | tf_op jit(solution)/shard_map/ppermute | solution.py:293
  48.5 6.2 %collective-permute-start.8 = (bf16[256,128]{1,0:T(8,128)(2,1)S(1)}, bf16[256,128]{1,0:T(8,128)(2,1)S(1)}, u32[]{:S(2)}, u32[]{:S(2)}) collective-permute-start(bf16[256,128]{1,0:T(8,128)(2,1)S(1)} %get-tuple-element.41), channel_id=1, source_target_pairs={{0,2},{1,3},{2,4},{3,5},{4,6},{5,7},{6,0},{7,1},{8,10},{9,11},{10,... | collective-permute-start | bytes 196616 | tf_op jit(solution)/shard_map/ppermute | solution.py:293
  51.2 6.3 %collective-permute-start.9 = (bf16[256,128]{1,0:T(8,128)(2,1)S(1)}, bf16[256,128]{1,0:T(8,128)(2,1)S(1)}, u32[]{:S(2)}, u32[]{:S(2)}) collective-permute-start(bf16[256,128]{1,0:T(8,128)(2,1)S(1)} %get-tuple-element.42), channel_id=1, source_target_pairs={{0,3},{1,4},{2,5},{3,6},{4,7},{5,0},{6,1},{7,2},{8,11},{9,12},{10,... | collective-permute-start | bytes 196616 | tf_op jit(solution)/shard_map/ppermute | solution.py:293
